TPU v7x, 512 devices: a whole 4x8x8 slice. The times are simulated.
512 devices in a mesh: blk: 32 (over x, z), batch: 16 (over y, core).
Axes of the slice: x: 4, y: 8, z: 8, core: 2. Of those that a mesh axis runs over, the one named last changes fastest.
Arguments:
- queries: bfloat16 [16, 8192, 2048], P('batch', 'blk'), may hold values from -8 to 8
- keys: bfloat16 [16, 8192, 1024], P('batch', 'blk'), may hold values from -8 to 8
- values: bfloat16 [16, 8192, 1024], P('batch', 'blk'), may hold values from -6 to 6
- seg_ids: int32 [16, 8192], P('batch', 'blk'), may hold values from 0 to 6, as said below
- lengths: int32 [16, 7], P('batch'), may hold values from 128 to 2048, as said below
- live: int32 [16, 32, 8], P('batch', 'blk'), may hold values from 0 to 1, as said below
- page_table: int32 [16, 7, 2], replicated, may hold values from 0 to 127, as said below
- pool: bfloat16 [128, 16, 2048], P('batch'), may hold values from -6 to 6
Outputs:
- attended: bfloat16 [16, 8192, 2048], P('batch', 'blk')
- cache_keys: bfloat16 [16, 8192, 1024], P('batch', 'blk')
Inputs may be any that keep to these rules, and one draw needn't show every extreme that they name: Each stream's lengths sum to 8192; one of them is exactly 2048, three lie between 1536 and 1920, and three between 128 and 512, in random order. seg_ids[b, t] is the prompt that token t falls in under lengths[b]: it never decreases and every prompt number appears. live[b, j, r - 1] is 1 exactly when j >= r and the first token of block j and the last token of block j - r have the same seg_ids. `page_table`: page p is held by index p // 8 of batch. Of one stream's 7 * 2 pages, at most 2 are held by any one index of batch, and exactly 2 by one of them in every stream.
All inputs are finite; a program needn't handle non-finite values.
Results may differ from a plain program's by a relative error of at most 0.0055.
The roundings to bfloat16 on the way count: a program that leaves them out, or rounds other values in their place, can miss the bound.
Values may be sent and summed in bfloat16 or wider, within the bound.
A program may use at most 128 MiB of HBM per device.

v0:
```python
import math

import jax
import jax.numpy as jnp
from jax import lax
from jax.sharding import PartitionSpec as P

QUERY_HEADS = 16
KEY_VALUE_HEADS = 8
HEAD_SIZE = 128


rope_base = 1000000.0


def shifted(value, axis, steps):
    count = lax.axis_size(axis)
    initial, last = (max(0, -steps), min(count, count - steps))
    return lax.ppermute(value, axis, [(source, source + steps) for source in range(initial, last)])


def apply_rotary(matrix, token_position, head_count):
    head_width = matrix.shape[-1] // head_count
    halfway = head_width // 2
    inverse = jnp.power(
        jnp.float32(rope_base), -2.0 * jnp.arange(halfway, dtype=jnp.float32) / head_width
    )
    angles = token_position.astype(jnp.float32)[:, None] * inverse[None, :]
    cosine = jnp.cos(angles)[:, None, :]
    sine_part = jnp.sin(angles)[:, None, :]
    split_heads = matrix.astype(jnp.float32).reshape(matrix.shape[0], head_count, head_width)
    leading = split_heads[..., :halfway]
    trailing = split_heads[..., halfway:]
    turned = jnp.concatenate(
        [leading * cosine - trailing * sine_part, trailing * cosine + leading * sine_part], axis=-1
    )
    return turned.reshape(matrix.shape[0], head_count * head_width).astype(jnp.bfloat16)


def segment_of(indices, lengths):
    seg_ends = jnp.cumsum(lengths)
    return jnp.sum((seg_ends[None, :] <= indices[:, None]).astype(jnp.int32), axis=1)


def positions(segment, lengths, offset, prefix_len):
    starts = jnp.cumsum(lengths) - lengths
    labels = jnp.arange(lengths.shape[0], dtype=jnp.int32)
    own_start = jnp.sum(jnp.where(segment[:, None] == labels[None, :], starts[None, :], 0), axis=1)
    token_index = offset + jnp.arange(segment.shape[0], dtype=jnp.int32)
    return prefix_len + token_index - own_start


def fold_block(state, query_heads, key_tile, value_tile, visible):
    highest, total, summed = state
    key_heads = key_tile.reshape(key_tile.shape[0], KEY_VALUE_HEADS, HEAD_SIZE)
    value_heads = value_tile.reshape(value_tile.shape[0], KEY_VALUE_HEADS, HEAD_SIZE)
    score = jnp.einsum(
        "thgd,uhd->hgtu", query_heads, key_heads, preferred_element_type=jnp.float32
    ) * (1.0 / math.sqrt(HEAD_SIZE))
    score = jnp.where(visible[None, None], score, -jnp.inf)
    new_high = jnp.maximum(highest, jnp.max(score, axis=-1))
    shrink = jnp.exp(highest - new_high)
    weight = jnp.exp(score - new_high[..., None])
    total = total * shrink + jnp.sum(weight, axis=-1)
    update = jnp.einsum(
        "hgtu,uhd->hgtd",
        weight.astype(jnp.bfloat16),
        value_heads,
        preferred_element_type=jnp.float32,
    )
    summed = summed * shrink[..., None] + update
    return (new_high, total, summed)


def per_device(queries, keys, values, seg_ids, lengths, live, page_table, pool):
    token_rows = queries.shape[1]
    q_width = queries.shape[2]
    kv_width = keys.shape[2]
    step_count = live.shape[2]
    column_count = lax.axis_size("batch")
    blk_index = lax.axis_index("blk")
    column = lax.axis_index("batch")
    pool_rows = pool.shape[0]
    page_tokens = pool.shape[1]
    page_floats = page_tokens * pool.shape[2]
    per_stream = page_table.shape[1] * page_table.shape[2]
    prefix_len = page_table.shape[2] * page_tokens
    capacity = max(2, (per_stream + column_count - 1) // column_count + 1)
    segment = seg_ids[0]
    own_lengths = lengths[0]
    block_start = blk_index * token_rows
    token_position = positions(segment, own_lengths, block_start, prefix_len)
    query_rotated = apply_rotary(queries[0], token_position, QUERY_HEADS)
    key_rotated = apply_rotary(keys[0], token_position, KEY_VALUE_HEADS)
    own_values = values[0]
    query_heads = query_rotated.reshape(
        token_rows, KEY_VALUE_HEADS, QUERY_HEADS // KEY_VALUE_HEADS, HEAD_SIZE
    )
    query_idx = block_start + jnp.arange(token_rows, dtype=jnp.int32)
    flat_table = page_table.reshape(page_table.shape[0], per_stream)
    holder = flat_table // pool_rows
    inside = flat_table % pool_rows
    order_ids = jnp.arange(per_stream, dtype=jnp.int32)
    ranking = jnp.sum(
        (
            (holder[:, None, :] == holder[:, :, None])
            & (order_ids[None, None, :] < order_ids[None, :, None])
        ).astype(jnp.int32),
        axis=2,
    )
    slot_ids = jnp.arange(capacity, dtype=jnp.int32)
    mine_holder = lax.dynamic_index_in_dim(holder, column, 0, keepdims=False)
    mine_rank = lax.dynamic_index_in_dim(ranking, column, 0, keepdims=False)
    receiver = (
        (mine_holder[:, None, None] == jnp.arange(column_count, dtype=jnp.int32)[None, :, None])
        & (mine_rank[:, None, None] == slot_ids[None, None, :])
    ).astype(jnp.bfloat16)
    flat_pool = pool.reshape(pool_rows, page_floats)
    picked = (holder == column)[:, :, None, None] & (
        ranking[:, :, None, None] == slot_ids[None, None, :, None]
    )
    picked = picked & (
        inside[:, :, None, None] == jnp.arange(pool_rows, dtype=jnp.int32)[None, None, None, :]
    )
    selector = jnp.sum(picked.astype(jnp.bfloat16), axis=1)
    arrived = lax.all_to_all(
        jnp.einsum("dcp,pf->dcf", selector, flat_pool, preferred_element_type=jnp.float32).astype(
            jnp.bfloat16
        ),
        "batch",
        split_axis=0,
        concat_axis=0,
        tiled=True,
    )
    prefix = jnp.einsum(
        "ksc,scf->kf", receiver, arrived, preferred_element_type=jnp.float32
    ).astype(jnp.bfloat16)
    prefix = prefix.reshape(per_stream * page_tokens, pool.shape[2])
    pre_keys = prefix[:, :kv_width]
    pre_values = prefix[:, kv_width:]
    pre_seg = jnp.arange(per_stream * page_tokens, dtype=jnp.int32) // prefix_len
    per_head_shape = (KEY_VALUE_HEADS, QUERY_HEADS // KEY_VALUE_HEADS, token_rows)
    state = (
        jnp.full(per_head_shape, -jnp.inf, jnp.float32),
        jnp.zeros(per_head_shape, jnp.float32),
        jnp.zeros(per_head_shape + (HEAD_SIZE,), jnp.float32),
    )
    state = fold_block(
        state, query_heads, pre_keys, pre_values, segment[:, None] == pre_seg[None, :]
    )

    def visible_to(key_first):
        key_idx = key_first + jnp.arange(token_rows, dtype=jnp.int32)
        key_seg = segment_of(key_idx, own_lengths)
        return (segment[:, None] == key_seg[None, :]) & (key_idx[None, :] <= query_idx[:, None])

    state = fold_block(state, query_heads, key_rotated, own_values, visible_to(block_start))
    live_steps = live[0, 0]

    def fold_far(state, distance, key_tile, value_tile):
        active = lax.dynamic_index_in_dim(live_steps, distance - 1, 0, keepdims=False) > 0
        return lax.cond(
            active,
            lambda inner: fold_block(
                inner,
                query_heads,
                key_tile,
                value_tile,
                visible_to(block_start - distance * token_rows),
            ),
            lambda inner: inner,
            state,
        )

    def one_hop(distance, carry):
        inner, key_tile, value_tile = carry
        key_tile, value_tile = shifted((key_tile, value_tile), "blk", 1)
        return (fold_far(inner, distance + 1, key_tile, value_tile), key_tile, value_tile)

    state = lax.fori_loop(0, step_count, one_hop, (state, key_rotated, own_values))[0]
    highest, total, summed = state
    result = summed / total[..., None]
    result = jnp.transpose(result, (2, 0, 1, 3)).reshape(token_rows, q_width).astype(jnp.bfloat16)
    return (result[None], key_rotated[None])


def solution(mesh):
    in_specs = (
        P("batch", "blk", None),
        P("batch", "blk", None),
        P("batch", "blk", None),
        P("batch", "blk"),
        P("batch", None),
        P("batch", "blk", None),
        P(),
        P("batch", None, None),
    )
    out_specs = (P("batch", "blk", None), P("batch", "blk", None))
    return jax.shard_map(
        per_device, mesh=mesh, in_specs=in_specs, out_specs=out_specs, check_vma=False
    )
```

profile of v0, /device:TPU:13, one launch (start us, length us, event | category | flops | bytes accessed | tf_op | source)
XLA Modules:
  0.0 376.8 jit_solution(8432542275295187456)
XLA Ops:
  6.2 3.5 copy.102
  9.7 8.0 %all-to-all-start = ((bf16[16,2,32768]{2,1,0:T(2,128)(2,1)}), bf16[16,2,32768]{2,1,0:T(2,128)(2,1)}, u32[]{:S(2)}, u32[]{:S(2)}) async-start(bf16[16,2,32768]{2,1,0:T(2,128)(2,1)} %copy.102), calls=%async_computation | async-start | bytes 4194304 | tf_op jit(solution)/shard_map/all_to_all | solution.py:126
  36.5 2.7 fusion.23
  39.1 26.1 %all-to-all-done = bf16[16,2,32768]{2,1,0:T(2,128)(2,1)} async-done(((bf16[16,2,32768]{2,1,0:T(2,128)(2,1)}), bf16[16,2,32768]{2,1,0:T(2,128)(2,1)}, u32[]{:S(2)}, u32[]{:S(2)}) %all-to-all-start) | async-done | bytes 2097184 | tf_op jit(solution)/shard_map/all_to_all | solution.py:126
  65.2 2.9 fusion.18
  76.6 296.8 %while.27 = (s32[]{:T(128)}, f32[8,2,256]{2,1,0:T(2,128)S(1)}, f32[8,2,256]{2,1,0:T(2,128)S(1)}, f32[8,2,256,128]{3,2,1,0:T(8,128)S(1)}, bf16[256,1024]{1,0:T(8,...) while((s32[]{:T(128)}, f32[8,2,256]{2,1,0:T(2,128)S(1)}, ...), condition=%wide.region_16.17_spmd.clone.clone, body=%wide.region_9.16_spmd.clone.clone.sunk | while | flops 549664256 | bytes 27798016 | solution.py:180
  76.6 4.0 %collective-permute-start = (bf16[256,1024]{1,0:T(8,128)(2,1)}, bf16[256,1024]{1,0:T(8,128)(2,1)}, u32[]{:S(2)}, u32[]{:S(2)}) collective-permute-start(bf16[256,1024]{1,0:T(8,128)(2,1)} %get-tuple-element.707), channel_id=1, source_target_pairs={{0,16},{16,32},{32,48},{48,64},{64,80},{80,96},{96,112},{112,128},... | collective-permute-start | bytes 1572872 | tf_op jit(solution)/shard_map/while/body/eval_jaxpr/ppermute | solution.py:19
  80.7 4.0 %collective-permute-start.1 = (bf16[256,1024]{1,0:T(8,128)(2,1)}, bf16[256,1024]{1,0:T(8,128)(2,1)}, u32[]{:S(2)}, u32[]{:S(2)}) collective-permute-start(bf16[256,1024]{1,0:T(8,128)(2,1)} %get-tuple-element.708), channel_id=1, source_target_pairs={{0,16},{16,32},{32,48},{48,64},{64,80},{80,96},{96,112},{112,128},... | collective-permute-start | bytes 1572872 | tf_op jit(solution)/shard_map/while/body/eval_jaxpr/ppermute | solution.py:19
  85.9 13.8 %collective-permute-done = bf16[256,1024]{1,0:T(8,128)(2,1)} collective-permute-done((bf16[256,1024]{1,0:T(8,128)(2,1)}, bf16[256,1024]{1,0:T(8,128)(2,1)}, u32[]{:S(2)}, u32[]{:S(2)}) %collective-permute-start) | collective-permute-done | bytes 524320 | tf_op jit(solution)/shard_map/while/body/eval_jaxpr/ppermute | solution.py:19
  99.8 11.2 %collective-permute-done.1 = bf16[256,1024]{1,0:T(8,128)(2,1)} collective-permute-done((bf16[256,1024]{1,0:T(8,128)(2,1)}, bf16[256,1024]{1,0:T(8,128)(2,1)}, u32[]{:S(2)}, u32[]{:S(2)}) %collective-permute-start.1) | collective-permute-done | bytes 524320 | tf_op jit(solution)/shard_map/while/body/eval_jaxpr/ppermute | solution.py:19
  111.0 6.4 %conditional.4 = ((f32[8,2,256]{2,1,0:T(2,128)S(1)}, f32[8,2,256]{2,1,0:T(2,128)S(1)}, f32[8,2,256,128]{3,2,1,0:T(8,128)S(1)})) conditional(s32[]{:T(128)} %bitcast.108, (f32[8,2,256]{2,1,0:T(2,128)S(1)}, f32[8,2,256]{2,1,0:T(2,128)S(1)}, f32[8,2,256,128]{3,2,1,0:T(8,128)S(1)}) %tuple.91, (s32[1,256]{1,0:T(1,128)S(1)}, s32[7]{0:T(128)S(1)}, ...), branch_computations={%region_10.10_spmd, %region_11.15_spmd} | conditional | flops 549664256 | bytes 21505176 | solution.py:162
  126.4 12.0 %collective-permute-done = bf16[256,1024]{1,0:T(8,128)(2,1)} collective-permute-done((bf16[256,1024]{1,0:T(8,128)(2,1)}, bf16[256,1024]{1,0:T(8,128)(2,1)}, u32[]{:S(2)}, u32[]{:S(2)}) %collective-permute-start) | collective-permute-done | bytes 524320 | tf_op jit(solution)/shard_map/while/body/eval_jaxpr/ppermute | solution.py:19
  138.4 11.2 %collective-permute-done.1 = bf16[256,1024]{1,0:T(8,128)(2,1)} collective-permute-done((bf16[256,1024]{1,0:T(8,128)(2,1)}, bf16[256,1024]{1,0:T(8,128)(2,1)}, u32[]{:S(2)}, u32[]{:S(2)}) %collective-permute-start.1) | collective-permute-done | bytes 524320 | tf_op jit(solution)/shard_map/while/body/eval_jaxpr/ppermute | solution.py:19
  149.6 6.4 %conditional.4 = ((f32[8,2,256]{2,1,0:T(2,128)S(1)}, f32[8,2,256]{2,1,0:T(2,128)S(1)}, f32[8,2,256,128]{3,2,1,0:T(8,128)S(1)})) conditional(s32[]{:T(128)} %bitcast.108, (f32[8,2,256]{2,1,0:T(2,128)S(1)}, f32[8,2,256]{2,1,0:T(2,128)S(1)}, f32[8,2,256,128]{3,2,1,0:T(8,128)S(1)}) %tuple.91, (s32[1,256]{1,0:T(1,128)S(1)}, s32[7]{0:T(128)S(1)}, ...), branch_computations={%region_10.10_spmd, %region_11.15_spmd} | conditional | flops 549664256 | bytes 21505176 | solution.py:162
  165.0 11.1 %collective-permute-done = bf16[256,1024]{1,0:T(8,128)(2,1)} collective-permute-done((bf16[256,1024]{1,0:T(8,128)(2,1)}, bf16[256,1024]{1,0:T(8,128)(2,1)}, u32[]{:S(2)}, u32[]{:S(2)}) %collective-permute-start) | collective-permute-done | bytes 524320 | tf_op jit(solution)/shard_map/while/body/eval_jaxpr/ppermute | solution.py:19
  176.2 11.2 %collective-permute-done.1 = bf16[256,1024]{1,0:T(8,128)(2,1)} collective-permute-done((bf16[256,1024]{1,0:T(8,128)(2,1)}, bf16[256,1024]{1,0:T(8,128)(2,1)}, u32[]{:S(2)}, u32[]{:S(2)}) %collective-permute-start.1) | collective-permute-done | bytes 524320 | tf_op jit(solution)/shard_map/while/body/eval_jaxpr/ppermute | solution.py:19
  187.4 6.4 %conditional.4 = ((f32[8,2,256]{2,1,0:T(2,128)S(1)}, f32[8,2,256]{2,1,0:T(2,128)S(1)}, f32[8,2,256,128]{3,2,1,0:T(8,128)S(1)})) conditional(s32[]{:T(128)} %bitcast.108, (f32[8,2,256]{2,1,0:T(2,128)S(1)}, f32[8,2,256]{2,1,0:T(2,128)S(1)}, f32[8,2,256,128]{3,2,1,0:T(8,128)S(1)}) %tuple.91, (s32[1,256]{1,0:T(1,128)S(1)}, s32[7]{0:T(128)S(1)}, ...), branch_computations={%region_10.10_spmd, %region_11.15_spmd} | conditional | flops 549664256 | bytes 21505176 | solution.py:162
  202.8 13.1 %collective-permute-done = bf16[256,1024]{1,0:T(8,128)(2,1)} collective-permute-done((bf16[256,1024]{1,0:T(8,128)(2,1)}, bf16[256,1024]{1,0:T(8,128)(2,1)}, u32[]{:S(2)}, u32[]{:S(2)}) %collective-permute-start) | collective-permute-done | bytes 524320 | tf_op jit(solution)/shard_map/while/body/eval_jaxpr/ppermute | solution.py:19
  215.9 7.4 %collective-permute-done.1 = bf16[256,1024]{1,0:T(8,128)(2,1)} collective-permute-done((bf16[256,1024]{1,0:T(8,128)(2,1)}, bf16[256,1024]{1,0:T(8,128)(2,1)}, u32[]{:S(2)}, u32[]{:S(2)}) %collective-permute-start.1) | collective-permute-done | bytes 524320 | tf_op jit(solution)/shard_map/while/body/eval_jaxpr/ppermute | solution.py:19
  223.3 6.4 %conditional.4 = ((f32[8,2,256]{2,1,0:T(2,128)S(1)}, f32[8,2,256]{2,1,0:T(2,128)S(1)}, f32[8,2,256,128]{3,2,1,0:T(8,128)S(1)})) conditional(s32[]{:T(128)} %bitcast.108, (f32[8,2,256]{2,1,0:T(2,128)S(1)}, f32[8,2,256]{2,1,0:T(2,128)S(1)}, f32[8,2,256,128]{3,2,1,0:T(8,128)S(1)}) %tuple.91, (s32[1,256]{1,0:T(1,128)S(1)}, s32[7]{0:T(128)S(1)}, ...), branch_computations={%region_10.10_spmd, %region_11.15_spmd} | conditional | flops 549664256 | bytes 21505176 | solution.py:162
  238.7 12.4 %collective-permute-done = bf16[256,1024]{1,0:T(8,128)(2,1)} collective-permute-done((bf16[256,1024]{1,0:T(8,128)(2,1)}, bf16[256,1024]{1,0:T(8,128)(2,1)}, u32[]{:S(2)}, u32[]{:S(2)}) %collective-permute-start) | collective-permute-done | bytes 524320 | tf_op jit(solution)/shard_map/while/body/eval_jaxpr/ppermute | solution.py:19
  251.2 5.6 %collective-permute-done.1 = bf16[256,1024]{1,0:T(8,128)(2,1)} collective-permute-done((bf16[256,1024]{1,0:T(8,128)(2,1)}, bf16[256,1024]{1,0:T(8,128)(2,1)}, u32[]{:S(2)}, u32[]{:S(2)}) %collective-permute-start.1) | collective-permute-done | bytes 524320 | tf_op jit(solution)/shard_map/while/body/eval_jaxpr/ppermute | solution.py:19
  256.8 6.4 %conditional.4 = ((f32[8,2,256]{2,1,0:T(2,128)S(1)}, f32[8,2,256]{2,1,0:T(2,128)S(1)}, f32[8,2,256,128]{3,2,1,0:T(8,128)S(1)})) conditional(s32[]{:T(128)} %bitcast.108, (f32[8,2,256]{2,1,0:T(2,128)S(1)}, f32[8,2,256]{2,1,0:T(2,128)S(1)}, f32[8,2,256,128]{3,2,1,0:T(8,128)S(1)}) %tuple.91, (s32[1,256]{1,0:T(1,128)S(1)}, s32[7]{0:T(128)S(1)}, ...), branch_computations={%region_10.10_spmd, %region_11.15_spmd} | conditional | flops 549664256 | bytes 21505176 | solution.py:162
  272.2 11.6 %collective-permute-done = bf16[256,1024]{1,0:T(8,128)(2,1)} collective-permute-done((bf16[256,1024]{1,0:T(8,128)(2,1)}, bf16[256,1024]{1,0:T(8,128)(2,1)}, u32[]{:S(2)}, u32[]{:S(2)}) %collective-permute-start) | collective-permute-done | bytes 524320 | tf_op jit(solution)/shard_map/while/body/eval_jaxpr/ppermute | solution.py:19
  283.8 5.6 %collective-permute-done.1 = bf16[256,1024]{1,0:T(8,128)(2,1)} collective-permute-done((bf16[256,1024]{1,0:T(8,128)(2,1)}, bf16[256,1024]{1,0:T(8,128)(2,1)}, u32[]{:S(2)}, u32[]{:S(2)}) %collective-permute-start.1) | collective-permute-done | bytes 524320 | tf_op jit(solution)/shard_map/while/body/eval_jaxpr/ppermute | solution.py:19
  289.4 6.4 %conditional.4 = ((f32[8,2,256]{2,1,0:T(2,128)S(1)}, f32[8,2,256]{2,1,0:T(2,128)S(1)}, f32[8,2,256,128]{3,2,1,0:T(8,128)S(1)})) conditional(s32[]{:T(128)} %bitcast.108, (f32[8,2,256]{2,1,0:T(2,128)S(1)}, f32[8,2,256]{2,1,0:T(2,128)S(1)}, f32[8,2,256,128]{3,2,1,0:T(8,128)S(1)}) %tuple.91, (s32[1,256]{1,0:T(1,128)S(1)}, s32[7]{0:T(128)S(1)}, ...), branch_computations={%region_10.10_spmd, %region_11.15_spmd} | conditional | flops 549664256 | bytes 21505176 | solution.py:162
  304.8 16.1 %collective-permute-done = bf16[256,1024]{1,0:T(8,128)(2,1)} collective-permute-done((bf16[256,1024]{1,0:T(8,128)(2,1)}, bf16[256,1024]{1,0:T(8,128)(2,1)}, u32[]{:S(2)}, u32[]{:S(2)}) %collective-permute-start) | collective-permute-done | bytes 524320 | tf_op jit(solution)/shard_map/while/body/eval_jaxpr/ppermute | solution.py:19
  320.9 5.6 %collective-permute-done.1 = bf16[256,1024]{1,0:T(8,128)(2,1)} collective-permute-done((bf16[256,1024]{1,0:T(8,128)(2,1)}, bf16[256,1024]{1,0:T(8,128)(2,1)}, u32[]{:S(2)}, u32[]{:S(2)}) %collective-permute-start.1) | collective-permute-done | bytes 524320 | tf_op jit(solution)/shard_map/while/body/eval_jaxpr/ppermute | solution.py:19
  326.5 6.4 %conditional.4 = ((f32[8,2,256]{2,1,0:T(2,128)S(1)}, f32[8,2,256]{2,1,0:T(2,128)S(1)}, f32[8,2,256,128]{3,2,1,0:T(8,128)S(1)})) conditional(s32[]{:T(128)} %bitcast.108, (f32[8,2,256]{2,1,0:T(2,128)S(1)}, f32[8,2,256]{2,1,0:T(2,128)S(1)}, f32[8,2,256,128]{3,2,1,0:T(8,128)S(1)}) %tuple.91, (s32[1,256]{1,0:T(1,128)S(1)}, s32[7]{0:T(128)S(1)}, ...), branch_computations={%region_10.10_spmd, %region_11.15_spmd} | conditional | flops 549664256 | bytes 21505176 | solution.py:162
  341.9 15.6 %collective-permute-done = bf16[256,1024]{1,0:T(8,128)(2,1)} collective-permute-done((bf16[256,1024]{1,0:T(8,128)(2,1)}, bf16[256,1024]{1,0:T(8,128)(2,1)}, u32[]{:S(2)}, u32[]{:S(2)}) %collective-permute-start) | collective-permute-done | bytes 524320 | tf_op jit(solution)/shard_map/while/body/eval_jaxpr/ppermute | solution.py:19
  357.5 5.6 %collective-permute-done.1 = bf16[256,1024]{1,0:T(8,128)(2,1)} collective-permute-done((bf16[256,1024]{1,0:T(8,128)(2,1)}, bf16[256,1024]{1,0:T(8,128)(2,1)}, u32[]{:S(2)}, u32[]{:S(2)}) %collective-permute-start.1) | collective-permute-done | bytes 524320 | tf_op jit(solution)/shard_map/while/body/eval_jaxpr/ppermute | solution.py:19
  363.1 6.4 %conditional.4 = ((f32[8,2,256]{2,1,0:T(2,128)S(1)}, f32[8,2,256]{2,1,0:T(2,128)S(1)}, f32[8,2,256,128]{3,2,1,0:T(8,128)S(1)})) conditional(s32[]{:T(128)} %bitcast.108, (f32[8,2,256]{2,1,0:T(2,128)S(1)}, f32[8,2,256]{2,1,0:T(2,128)S(1)}, f32[8,2,256,128]{3,2,1,0:T(8,128)S(1)}) %tuple.91, (s32[1,256]{1,0:T(1,128)S(1)}, s32[7]{0:T(128)S(1)}, ...), branch_computations={%region_10.10_spmd, %region_11.15_spmd} | conditional | flops 549664256 | bytes 21505176 | solution.py:162
  (218 shorter events, 149.6 us)
Async XLA Ops:
  6.1 11.5 %copy-start.3 = (bf16[1,256,2048]{2,1,0:T(8,128)(2,1)S(1)}, bf16[1,256,2048]{2,1,0:T(8,128)(2,1)}, u32[]{:S(2)}) copy-start(bf16[1,256,2048]{2,1,0:T(8,128)(2,1)} %param.12) | copy-start | bytes 3145732
  9.7 9.6 %copy-start.4 = (bf16[1,256,1024]{2,1,0:T(8,128)(2,1)S(1)}, bf16[1,256,1024]{2,1,0:T(8,128)(2,1)}, u32[]{:S(2)}) copy-start(bf16[1,256,1024]{2,1,0:T(8,128)(2,1)} %param.13) | copy-start | bytes 1572868
  9.7 55.6 %all-to-all-start = ((bf16[16,2,32768]{2,1,0:T(2,128)(2,1)}), bf16[16,2,32768]{2,1,0:T(2,128)(2,1)}, u32[]{:S(2)}, u32[]{:S(2)}) async-start(bf16[16,2,32768]{2,1,0:T(2,128)(2,1)} %copy.102), calls=%async_computation | async-start | bytes 4194304 | tf_op jit(solution)/shard_map/all_to_all | solution.py:126
  17.6 2.9 copy-start.7
  20.7 7.7 %copy-start.6 = (s32[1,256]{1,0:T(1,128)S(1)}, s32[1,256]{1,0:T(1,128)}, u32[]{:S(2)}) copy-start(s32[1,256]{1,0:T(1,128)} %param.15) | copy-start | bytes 3076
  30.9 3.3 copy-start.1
  34.2 2.3 copy-start.2
  69.2 2.2 copy-start
  69.4 2.9 copy-start.5
  74.5 2.2 copy-start.8
  76.6 23.1 %collective-permute-start = (bf16[256,1024]{1,0:T(8,128)(2,1)}, bf16[256,1024]{1,0:T(8,128)(2,1)}, u32[]{:S(2)}, u32[]{:S(2)}) collective-permute-start(bf16[256,1024]{1,0:T(8,128)(2,1)} %get-tuple-element.707), channel_id=1, source_target_pairs={{0,16},{16,32},{32,48},{48,64},{64,80},{80,96},{96,112},{112,128},... | collective-permute-start | bytes 1572872 | tf_op jit(solution)/shard_map/while/body/eval_jaxpr/ppermute | solution.py:19
  80.7 30.4 %collective-permute-start.1 = (bf16[256,1024]{1,0:T(8,128)(2,1)}, bf16[256,1024]{1,0:T(8,128)(2,1)}, u32[]{:S(2)}, u32[]{:S(2)}) collective-permute-start(bf16[256,1024]{1,0:T(8,128)(2,1)} %get-tuple-element.708), channel_id=1, source_target_pairs={{0,16},{16,32},{32,48},{48,64},{64,80},{80,96},{96,112},{112,128},... | collective-permute-start | bytes 1572872 | tf_op jit(solution)/shard_map/while/body/eval_jaxpr/ppermute | solution.py:19
  121.3 17.1 %collective-permute-start = (bf16[256,1024]{1,0:T(8,128)(2,1)}, bf16[256,1024]{1,0:T(8,128)(2,1)}, u32[]{:S(2)}, u32[]{:S(2)}) collective-permute-start(bf16[256,1024]{1,0:T(8,128)(2,1)} %get-tuple-element.707), channel_id=1, source_target_pairs={{0,16},{16,32},{32,48},{48,64},{64,80},{80,96},{96,112},{112,128},... | collective-permute-start | bytes 1572872 | tf_op jit(solution)/shard_map/while/body/eval_jaxpr/ppermute | solution.py:19
  123.2 26.4 %collective-permute-start.1 = (bf16[256,1024]{1,0:T(8,128)(2,1)}, bf16[256,1024]{1,0:T(8,128)(2,1)}, u32[]{:S(2)}, u32[]{:S(2)}) collective-permute-start(bf16[256,1024]{1,0:T(8,128)(2,1)} %get-tuple-element.708), channel_id=1, source_target_pairs={{0,16},{16,32},{32,48},{48,64},{64,80},{80,96},{96,112},{112,128},... | collective-permute-start | bytes 1572872 | tf_op jit(solution)/shard_map/while/body/eval_jaxpr/ppermute | solution.py:19
  159.9 16.2 %collective-permute-start = (bf16[256,1024]{1,0:T(8,128)(2,1)}, bf16[256,1024]{1,0:T(8,128)(2,1)}, u32[]{:S(2)}, u32[]{:S(2)}) collective-permute-start(bf16[256,1024]{1,0:T(8,128)(2,1)} %get-tuple-element.707), channel_id=1, source_target_pairs={{0,16},{16,32},{32,48},{48,64},{64,80},{80,96},{96,112},{112,128},... | collective-permute-start | bytes 1572872 | tf_op jit(solution)/shard_map/while/body/eval_jaxpr/ppermute | solution.py:19
  161.8 25.6 %collective-permute-start.1 = (bf16[256,1024]{1,0:T(8,128)(2,1)}, bf16[256,1024]{1,0:T(8,128)(2,1)}, u32[]{:S(2)}, u32[]{:S(2)}) collective-permute-start(bf16[256,1024]{1,0:T(8,128)(2,1)} %get-tuple-element.708), channel_id=1, source_target_pairs={{0,16},{16,32},{32,48},{48,64},{64,80},{80,96},{96,112},{112,128},... | collective-permute-start | bytes 1572872 | tf_op jit(solution)/shard_map/while/body/eval_jaxpr/ppermute | solution.py:19
  197.7 18.2 %collective-permute-start = (bf16[256,1024]{1,0:T(8,128)(2,1)}, bf16[256,1024]{1,0:T(8,128)(2,1)}, u32[]{:S(2)}, u32[]{:S(2)}) collective-permute-start(bf16[256,1024]{1,0:T(8,128)(2,1)} %get-tuple-element.707), channel_id=1, source_target_pairs={{0,16},{16,32},{32,48},{48,64},{64,80},{80,96},{96,112},{112,128},... | collective-permute-start | bytes 1572872 | tf_op jit(solution)/shard_map/while/body/eval_jaxpr/ppermute | solution.py:19
  199.6 23.7 %collective-permute-start.1 = (bf16[256,1024]{1,0:T(8,128)(2,1)}, bf16[256,1024]{1,0:T(8,128)(2,1)}, u32[]{:S(2)}, u32[]{:S(2)}) collective-permute-start(bf16[256,1024]{1,0:T(8,128)(2,1)} %get-tuple-element.708), channel_id=1, source_target_pairs={{0,16},{16,32},{32,48},{48,64},{64,80},{80,96},{96,112},{112,128},... | collective-permute-start | bytes 1572872 | tf_op jit(solution)/shard_map/while/body/eval_jaxpr/ppermute | solution.py:19
  233.6 17.6 %collective-permute-start = (bf16[256,1024]{1,0:T(8,128)(2,1)}, bf16[256,1024]{1,0:T(8,128)(2,1)}, u32[]{:S(2)}, u32[]{:S(2)}) collective-permute-start(bf16[256,1024]{1,0:T(8,128)(2,1)} %get-tuple-element.707), channel_id=1, source_target_pairs={{0,16},{16,32},{32,48},{48,64},{64,80},{80,96},{96,112},{112,128},... | collective-permute-start | bytes 1572872 | tf_op jit(solution)/shard_map/while/body/eval_jaxpr/ppermute | solution.py:19
  235.5 21.3 %collective-permute-start.1 = (bf16[256,1024]{1,0:T(8,128)(2,1)}, bf16[256,1024]{1,0:T(8,128)(2,1)}, u32[]{:S(2)}, u32[]{:S(2)}) collective-permute-start(bf16[256,1024]{1,0:T(8,128)(2,1)} %get-tuple-element.708), channel_id=1, source_target_pairs={{0,16},{16,32},{32,48},{48,64},{64,80},{80,96},{96,112},{112,128},... | collective-permute-start | bytes 1572872 | tf_op jit(solution)/shard_map/while/body/eval_jaxpr/ppermute | solution.py:19
  267.1 16.7 %collective-permute-start = (bf16[256,1024]{1,0:T(8,128)(2,1)}, bf16[256,1024]{1,0:T(8,128)(2,1)}, u32[]{:S(2)}, u32[]{:S(2)}) collective-permute-start(bf16[256,1024]{1,0:T(8,128)(2,1)} %get-tuple-element.707), channel_id=1, source_target_pairs={{0,16},{16,32},{32,48},{48,64},{64,80},{80,96},{96,112},{112,128},... | collective-permute-start | bytes 1572872 | tf_op jit(solution)/shard_map/while/body/eval_jaxpr/ppermute | solution.py:19
  269.0 20.4 %collective-permute-start.1 = (bf16[256,1024]{1,0:T(8,128)(2,1)}, bf16[256,1024]{1,0:T(8,128)(2,1)}, u32[]{:S(2)}, u32[]{:S(2)}) collective-permute-start(bf16[256,1024]{1,0:T(8,128)(2,1)} %get-tuple-element.708), channel_id=1, source_target_pairs={{0,16},{16,32},{32,48},{48,64},{64,80},{80,96},{96,112},{112,128},... | collective-permute-start | bytes 1572872 | tf_op jit(solution)/shard_map/while/body/eval_jaxpr/ppermute | solution.py:19
  299.7 21.2 %collective-permute-start = (bf16[256,1024]{1,0:T(8,128)(2,1)}, bf16[256,1024]{1,0:T(8,128)(2,1)}, u32[]{:S(2)}, u32[]{:S(2)}) collective-permute-start(bf16[256,1024]{1,0:T(8,128)(2,1)} %get-tuple-element.707), channel_id=1, source_target_pairs={{0,16},{16,32},{32,48},{48,64},{64,80},{80,96},{96,112},{112,128},... | collective-permute-start | bytes 1572872 | tf_op jit(solution)/shard_map/while/body/eval_jaxpr/ppermute | solution.py:19
  301.6 24.9 %collective-permute-start.1 = (bf16[256,1024]{1,0:T(8,128)(2,1)}, bf16[256,1024]{1,0:T(8,128)(2,1)}, u32[]{:S(2)}, u32[]{:S(2)}) collective-permute-start(bf16[256,1024]{1,0:T(8,128)(2,1)} %get-tuple-element.708), channel_id=1, source_target_pairs={{0,16},{16,32},{32,48},{48,64},{64,80},{80,96},{96,112},{112,128},... | collective-permute-start | bytes 1572872 | tf_op jit(solution)/shard_map/while/body/eval_jaxpr/ppermute | solution.py:19
  336.8 20.8 %collective-permute-start = (bf16[256,1024]{1,0:T(8,128)(2,1)}, bf16[256,1024]{1,0:T(8,128)(2,1)}, u32[]{:S(2)}, u32[]{:S(2)}) collective-permute-start(bf16[256,1024]{1,0:T(8,128)(2,1)} %get-tuple-element.707), channel_id=1, source_target_pairs={{0,16},{16,32},{32,48},{48,64},{64,80},{80,96},{96,112},{112,128},... | collective-permute-start | bytes 1572872 | tf_op jit(solution)/shard_map/while/body/eval_jaxpr/ppermute | solution.py:19
  338.7 24.5 %collective-permute-start.1 = (bf16[256,1024]{1,0:T(8,128)(2,1)}, bf16[256,1024]{1,0:T(8,128)(2,1)}, u32[]{:S(2)}, u32[]{:S(2)}) collective-permute-start(bf16[256,1024]{1,0:T(8,128)(2,1)} %get-tuple-element.708), channel_id=1, source_target_pairs={{0,16},{16,32},{32,48},{48,64},{64,80},{80,96},{96,112},{112,128},... | collective-permute-start | bytes 1572872 | tf_op jit(solution)/shard_map/while/body/eval_jaxpr/ppermute | solution.py:19
where the time goes:
time: 379 us; the launch traced here: 377 us
  waiting for transfers between devices  195 us (51%)
  local copies, waits for them, and re-layouts  79.4 us (21%)
  starting transfers between devices  42.8 us (11%)
  matrix products  32.4 us (9%)
  other arithmetic  20 us (5%)
  loops' own time  5.78 us (2%)
    ppermute x16, waiting for transfers between devices, shifted(): lax.ppermute(value, axis, [(source, source + steps) for source in range(i...  169 us
    ppermute x16, starting transfers between devices, shifted(): lax.ppermute(value, axis, [(source, source + steps) for source in range(i...  34.8 us
    while x16, local copies, waits for them, and re-layouts  30.9 us
    all_to_all x1, waiting for transfers between devices, per_device(): lax.all_to_all(jnp.einsum('dcp,pf->dcf', selector, flat_pool, preferred_e...  26.1 us
    dot_general x10, matrix products, fold_block(): jnp.einsum('hgtu,uhd->hgtd', weight.astype(jnp.bfloat16), value_heads, pr...  19.4 us
    cond x24, local copies, waits for them, and re-layouts  18.2 us
    unnamed x29, local copies, waits for them, and re-layouts  13.4 us
    dot_general x10, matrix products, fold_block(): jnp.einsum('thgd,uhd->hgtu', query_heads, key_heads, preferred_element_ty...  9.42 us
  transfers between devices with their start and end apart: 17, of which 17 were waited for; matrix products, arithmetic and copies ran while one was open for 7% of the time, Pallas kernels for 0%

commit v1 on v0

v1 whole, which is shorter than its diff:
```python
import math

import jax
import jax.numpy as jnp
import numpy as np
from jax import lax
from jax.experimental import pallas as pl
from jax.experimental.pallas import tpu as pltpu
from jax.sharding import PartitionSpec as P

HEAD = 128
KV_HEADS = 8
RING = 8
TOK = 256
SEGS = 7
PAGES_SEG = 2
PAGE = 16
PREFIX = PAGES_SEG * PAGE
PAIR = 2 * HEAD
ROPE_BASE = 1000000.0
LOG2E_SCALE = math.log2(math.e) / math.sqrt(HEAD)
NEG = -1e30
MESH = pl.DeviceIdType.MESH


def kernel(
    n_x,
    n_batch,
    pool_rows,
    queries,
    keys,
    values,
    lengths,
    page_table,
    pool,
    freq,
    attended,
    cache,
    qrot,
    krot,
    qbuf,
    kvbuf,
    pbuf,
    pown,
    pre,
    scores,
    q2,
    obuf,
    v_send,
    v_recv,
    k_send,
    k_recv,
    q_send,
    q_recv,
    f_send,
    f_recv,
    p_send,
    p_recv,
    o_send,
    o_recv,
    local,
):
    blk = lax.axis_index("blk")
    bat = lax.axis_index("batch")
    z = lax.rem(blk, RING)
    x = lax.div(blk, RING)

    def ring(d):
        return lax.rem(z + d, RING)

    def ring_id(d):
        return (x * RING + ring(d), bat)

    def other(e):
        return lax.rem(bat + e, n_batch)

    def lanes(i, width):
        return pl.ds(pl.multiple_of(i * width, width), width)

    def rows(i):
        return pl.ds(pl.multiple_of(i * TOK, TOK), TOK)

    ahead = (lax.rem(x + 1, n_x) * RING + z, bat)
    behind = (lax.rem(x + n_x - 1, n_x) * RING + z, bat)

    barrier = pltpu.get_barrier_semaphore()
    for d in range(1, RING):
        pl.semaphore_signal(barrier, inc=1, device_id=ring_id(d), device_id_type=MESH)
    for who in (ahead, behind):
        pl.semaphore_signal(barrier, inc=1, device_id=who, device_id_type=MESH)
    for e in range(1, n_batch):
        pl.semaphore_signal(barrier, inc=1, device_id=(blk, other(e)), device_id_type=MESH)
    own_pool_k = pltpu.make_async_copy(pool.at[:, :, lanes(z, HEAD)], pown.at[:, :, 0:HEAD], local.at[0])
    own_pool_v = pltpu.make_async_copy(
        pool.at[:, :, lanes(z + KV_HEADS, HEAD)], pown.at[:, :, HEAD:PAIR], local.at[1]
    )
    own_v = pltpu.make_async_copy(
        values.at[0, :, lanes(z, HEAD)], kvbuf.at[rows(RING + z), HEAD:PAIR], local.at[2]
    )
    own_pool_k.start()
    own_pool_v.start()
    own_v.start()
    pl.semaphore_wait(barrier, RING - 1 + 2 + n_batch - 1)

    def send_v(d):
        return pltpu.make_async_remote_copy(
            src_ref=values.at[0, :, lanes(ring(d), HEAD)],
            dst_ref=kvbuf.at[rows(RING + z), HEAD:PAIR],
            send_sem=v_send.at[d],
            recv_sem=v_recv.at[d],
            device_id=ring_id(d),
            device_id_type=MESH,
        )

    def send_k(d):
        return pltpu.make_async_remote_copy(
            src_ref=krot.at[:, lanes(ring(d), HEAD)],
            dst_ref=kvbuf.at[rows(RING + z), 0:HEAD],
            send_sem=k_send.at[d],
            recv_sem=k_recv.at[d],
            device_id=ring_id(d),
            device_id_type=MESH,
        )

    def send_q(d):
        return pltpu.make_async_remote_copy(
            src_ref=qrot.at[:, lanes(ring(d), PAIR)],
            dst_ref=qbuf.at[z],
            send_sem=q_send.at[d],
            recv_sem=q_recv.at[d],
            device_id=ring_id(d),
            device_id_type=MESH,
        )

    def send_pool(e):
        return pltpu.make_async_remote_copy(
            src_ref=pown,
            dst_ref=pbuf.at[pl.ds(bat * pool_rows, pool_rows)],
            send_sem=p_send.at[e],
            recv_sem=p_recv.at[e],
            device_id=(blk, other(e)),
            device_id_type=MESH,
        )

    def forward(s):
        return pltpu.make_async_remote_copy(
            src_ref=kvbuf.at[rows(RING + s)],
            dst_ref=kvbuf.at[rows(s)],
            send_sem=f_send.at[s],
            recv_sem=f_recv.at[s],
            device_id=ahead,
            device_id_type=MESH,
        )

    def send_o(d):
        return pltpu.make_async_remote_copy(
            src_ref=obuf.at[d],
            dst_ref=attended.at[0, :, lanes(z, PAIR)],
            send_sem=o_send.at[d],
            recv_sem=o_recv.at[d],
            device_id=ring_id(RING - d),
            device_id_type=MESH,
        )

    near = (1, 7, 2, 6, 3, 5, 4)
    for d in near:
        send_v(d).start()
    own_pool_k.wait()
    own_pool_v.wait()
    for e in range(1, n_batch):
        send_pool(e).start()
    own_pool = pltpu.make_async_copy(pown, pbuf.at[pl.ds(bat * pool_rows, pool_rows)], local.at[0])
    own_pool.start()

    starts = [jnp.int32(0)]
    for s in range(SEGS - 1):
        starts.append(starts[-1] + lengths[0, s])

    def start_and_segment(token):
        first = jnp.zeros_like(token)
        segment = jnp.zeros_like(token)
        for s in range(1, SEGS):
            inside = token >= starts[s]
            first = jnp.where(inside, starts[s], first)
            segment = jnp.where(inside, s, segment)
        return first, segment

    row = lax.broadcasted_iota(jnp.int32, (TOK, HEAD), 0)
    lane = lax.broadcasted_iota(jnp.int32, (TOK, HEAD), 1)
    token = row + blk * TOK
    first, _ = start_and_segment(token)
    angle = (PREFIX + token - first).astype(jnp.float32) * freq[0:1, :]
    cosine = jnp.cos(angle)
    sine = jnp.sin(angle)
    sine = jnp.where(lane < HEAD // 2, -sine, sine)

    def turn(part):
        part = part.astype(jnp.float32)
        return (part * cosine + pltpu.roll(part, HEAD // 2, 1) * sine).astype(jnp.bfloat16)

    for h in range(KV_HEADS):
        krot[:, h * HEAD : (h + 1) * HEAD] = turn(keys[0, :, h * HEAD : (h + 1) * HEAD])
    for d in near:
        send_k(d).start()
    own_k = pltpu.make_async_copy(
        krot.at[:, lanes(z, HEAD)], kvbuf.at[rows(RING + z), 0:HEAD], local.at[1]
    )
    own_k.start()
    cache_copy = pltpu.make_async_copy(krot, cache.at[0], local.at[3])
    cache_copy.start()
    for h in range(2 * KV_HEADS):
        qrot[:, h * HEAD : (h + 1) * HEAD] = turn(queries[0, :, h * HEAD : (h + 1) * HEAD])
    for d in near:
        send_q(d).start()
    own_q = pltpu.make_async_copy(qrot.at[:, lanes(z, PAIR)], qbuf.at[z], local.at[4])
    own_q.start()

    own_v.wait()
    own_k.wait()
    forward(z).start()

    def from_ring(sem, width_lo, d):
        src = ring(RING - d)
        view = kvbuf.at[rows(RING + src), width_lo : width_lo + HEAD]
        return pltpu.make_async_remote_copy(
            src_ref=view,
            dst_ref=view,
            send_sem=v_send.at[d],
            recv_sem=sem.at[d],
            device_id=ring_id(RING - d),
            device_id_type=MESH,
        )

    for d in near:
        from_ring(v_recv, HEAD, d).wait_recv()
        from_ring(k_recv, 0, d).wait_recv()
        forward(ring(RING - d)).start()

    own_pool.wait()
    for e in range(1, n_batch):
        src = pl.ds(lax.rem(bat + n_batch - e, n_batch) * pool_rows, pool_rows)
        pltpu.make_async_remote_copy(
            src_ref=pown,
            dst_ref=pbuf.at[src],
            send_sem=p_send.at[e],
            recv_sem=p_recv.at[e],
            device_id=(blk, other(n_batch - e)),
            device_id_type=MESH,
        ).wait_recv()
    for s in range(SEGS):
        for i in range(PAGES_SEG):
            at = s * PREFIX + i * PAGE
            pre[at : at + PAGE, :] = pbuf[page_table[bat, s, i]]
    pre[SEGS * PREFIX :, :] = jnp.zeros((TOK - SEGS * PREFIX, PAIR), jnp.bfloat16)

    for s in range(RING):
        forward(s).wait_recv()

    row2 = lax.rem(lax.broadcasted_iota(jnp.int32, (2 * TOK, HEAD), 0), TOK)
    lane2 = lax.broadcasted_iota(jnp.int32, (2 * TOK, HEAD), 1)
    contract_last = (((1,), (1,)), ((), ()))

    def one_block(i, carry):
        odd = lax.rem(i, 2)
        half = lax.div(i + 1, 2)
        d = lax.rem(odd * half + (1 - odd) * (RING - half), RING)
        src = ring(RING - d)

        @pl.when(i == 0)
        def _():
            pltpu.make_async_copy(qrot.at[:, lanes(z, PAIR)], qbuf.at[z], local.at[4]).wait()

        @pl.when(i > 0)
        def _():
            pltpu.make_async_remote_copy(
                src_ref=qbuf.at[src],
                dst_ref=qbuf.at[src],
                send_sem=q_send.at[d],
                recv_sem=q_recv.at[d],
                device_id=ring_id(RING - d),
                device_id_type=MESH,
            ).wait_recv()

        q2[0:TOK, :] = qbuf[src, :, 0:HEAD]
        q2[TOK : 2 * TOK, :] = qbuf[src, :, HEAD:PAIR]
        block0 = (x * RING + src) * TOK
        begin, segment = start_and_segment(row2 + block0)
        limit = begin - lane2 - (block0 - RING * TOK)
        causal = row2 - lane2
        segment_at = segment * PREFIX - lane2
        highest = jnp.full((2 * TOK, HEAD), NEG, jnp.float32)
        for c in range(RING + 2):
            if c <= RING:
                tile = kvbuf[rows(src + c), 0:HEAD]
            else:
                tile = pre[:, 0:HEAD]
            score = lax.dot_general(
                q2[...], tile, contract_last, preferred_element_type=jnp.float32
            )
            for part in range(2):
                at = part * HEAD
                if c < RING:
                    seen = limit <= c * TOK + at
                elif c == RING:
                    seen = (limit <= c * TOK + at) & (causal >= at)
                else:
                    seen = (segment_at <= at) & (segment_at > at - PREFIX)
                piece = jnp.where(seen, score[:, at : at + HEAD], NEG)
                highest = jnp.maximum(highest, piece)
                scores[c, :, at : at + HEAD] = piece
        top = jnp.max(highest, axis=1, keepdims=True)
        total = jnp.zeros((2 * TOK, HEAD), jnp.float32)
        summed = jnp.zeros((2 * TOK, HEAD), jnp.float32)
        for c in range(RING + 2):
            weight = jnp.exp2((scores[c] - top) * LOG2E_SCALE)
            total = total + (weight[:, 0:HEAD] + weight[:, HEAD:PAIR])
            if c <= RING:
                tile = kvbuf[rows(src + c), HEAD:PAIR]
            else:
                tile = pre[:, HEAD:PAIR]
            summed = summed + jnp.dot(
                weight.astype(jnp.bfloat16), tile, preferred_element_type=jnp.float32
            )
        result = (summed / jnp.sum(total, axis=1, keepdims=True)).astype(jnp.bfloat16)
        obuf[d, :, 0:HEAD] = result[0:TOK]
        obuf[d, :, HEAD:PAIR] = result[TOK : 2 * TOK]

        @pl.when(i == 0)
        def _():
            pltpu.make_async_copy(
                obuf.at[0], attended.at[0, :, lanes(z, PAIR)], local.at[2]
            ).start()

        @pl.when(i > 0)
        def _():
            send_o(d).start()

        return carry

    lax.fori_loop(0, RING, one_block, 0)

    for d in range(1, RING):
        send_v(d).wait_send()
        send_k(d).wait_send()
        send_q(d).wait_send()
    for s in range(RING):
        forward(s).wait_send()
    for e in range(1, n_batch):
        send_pool(e).wait_send()
    cache_copy.wait()
    pltpu.make_async_copy(obuf.at[0], attended.at[0, :, lanes(z, PAIR)], local.at[2]).wait()
    for d in range(1, RING):
        send_o(d).wait_send()
        pltpu.make_async_remote_copy(
            src_ref=obuf.at[d],
            dst_ref=attended.at[0, :, lanes(ring(d), PAIR)],
            send_sem=o_send.at[d],
            recv_sem=o_recv.at[d],
            device_id=ring_id(d),
            device_id_type=MESH,
        ).wait_recv()


def per_device(queries, keys, values, seg_ids, lengths, live, page_table, pool):
    n_x = lax.axis_size("blk") // RING
    n_batch = lax.axis_size("batch")
    pool_rows = pool.shape[0]
    half = HEAD // 2
    inverse = np.power(np.float64(ROPE_BASE), -2.0 * np.arange(half) / HEAD)
    freq = jnp.asarray(np.tile(np.concatenate([inverse, inverse])[None], (8, 1)), jnp.float32)

    def body(*refs):
        kernel(n_x, n_batch, pool_rows, *refs)

    bf = jnp.bfloat16
    dma = pltpu.SemaphoreType.DMA
    vmem = pl.BlockSpec(memory_space=pltpu.VMEM)
    smem = pl.BlockSpec(memory_space=pltpu.SMEM)
    anywhere = pl.BlockSpec(memory_space=pl.ANY)
    return pl.pallas_call(
        body,
        out_shape=(
            jax.ShapeDtypeStruct(queries.shape, bf),
            jax.ShapeDtypeStruct(keys.shape, bf),
        ),
        in_specs=[vmem, vmem, anywhere, smem, smem, anywhere, vmem],
        out_specs=(anywhere, anywhere),
        scratch_shapes=[
            pltpu.VMEM((TOK, 2 * KV_HEADS * HEAD), bf),
            pltpu.VMEM((TOK, KV_HEADS * HEAD), bf),
            pltpu.VMEM((RING, TOK, PAIR), bf),
            pltpu.VMEM((2 * RING * TOK, PAIR), bf),
            pltpu.VMEM((n_batch * pool_rows, PAGE, PAIR), bf),
            pltpu.VMEM((pool_rows, PAGE, PAIR), bf),
            pltpu.VMEM((TOK, PAIR), bf),
            pltpu.VMEM((RING + 2, 2 * TOK, TOK), jnp.float32),
            pltpu.VMEM((2 * TOK, HEAD), bf),
            pltpu.VMEM((RING, TOK, PAIR), bf),
            dma((RING,)),
            dma((RING,)),
            dma((RING,)),
            dma((RING,)),
            dma((RING,)),
            dma((RING,)),
            dma((RING,)),
            dma((RING,)),
            dma((n_batch,)),
            dma((n_batch,)),
            dma((RING,)),
            dma((RING,)),
            dma((5,)),
        ],
        compiler_params=pltpu.CompilerParams(
            collective_id=0, has_side_effects=True, vmem_limit_bytes=48 * 1024 * 1024
        ),
    )(queries, keys, values, lengths, page_table, pool, freq)


def solution(mesh):
    in_specs = (
        P("batch", "blk", None),
        P("batch", "blk", None),
        P("batch", "blk", None),
        P("batch", "blk"),
        P("batch", None),
        P("batch", "blk", None),
        P(),
        P("batch", None, None),
    )
    out_specs = (P("batch", "blk", None), P("batch", "blk", None))
    return jax.shard_map(
        per_device, mesh=mesh, in_specs=in_specs, out_specs=out_specs, check_vma=False
    )
```

time: 379 us -> 103 us (0.27)
  the two profiles are of different devices: /device:TPU:13 before, /device:TPU:1 now
where the time goes in v1:
time: 103 us; the launch traced here: 102 us
  Pallas kernels  93.9 us (91%)
  local copies, waits for them, and re-layouts  6.94 us (7%)
    pallas_call x1, Pallas kernels, per_device(): pl.pallas_call(body, out_shape=(jax.ShapeDtypeStruct(queries.shape, bf),...  93.9 us
    unnamed x15, local copies, waits for them, and re-layouts  6.94 us

profile of v1, /device:TPU:1, one launch (start us, length us, event | category | flops | bytes accessed | tf_op | source)
XLA Modules:
  0.0 101.5 jit_solution(17410603341116611175)
XLA Ops:
  0.6 0.0 copy-start.4
  0.6 0.0 copy-start.5
  0.7 0.8 copy.9.refs_4_
  1.5 0.0 copy-done.4
  1.5 0.0 copy-done.5
  1.5 0.0 copy-start
  1.5 1.2 %copy-done = bf16[1,256,2048]{2,1,0:T(8,128)(2,1)S(1)} copy-done((bf16[1,256,2048]{2,1,0:T(8,128)(2,1)S(1)}, bf16[1,256,2048]{2,1,0:T(8,128)(2,1)}, u32[]{:S(2)}) %copy-start) | copy-done | bytes 1048600
  2.7 0.0 copy-start.1
  2.7 1.0 %copy-done.1 = bf16[1,256,1024]{2,1,0:T(8,128)(2,1)S(1)} copy-done((bf16[1,256,1024]{2,1,0:T(8,128)(2,1)S(1)}, bf16[1,256,1024]{2,1,0:T(8,128)(2,1)}, u32[]{:S(2)}) %copy-start.1) | copy-done | bytes 524312
  3.8 0.0 copy-start.2
  3.8 1.0 %copy-done.2 = bf16[1,256,1024]{2,1,0:T(8,128)(2,1)S(1)} copy-done((bf16[1,256,1024]{2,1,0:T(8,128)(2,1)S(1)}, bf16[1,256,1024]{2,1,0:T(8,128)(2,1)}, u32[]{:S(2)}) %copy-start.2) | copy-done | bytes 524312
  4.8 0.0 copy-start.3
  4.8 1.0 %copy-done.3 = bf16[8,16,2048]{2,1,0:T(8,128)(2,1)S(1)} copy-done((bf16[8,16,2048]{2,1,0:T(8,128)(2,1)S(1)}, bf16[8,16,2048]{2,1,0:T(8,128)(2,1)}, u32[]{:S(2)}) %copy-start.3) | copy-done | bytes 524312
  5.8 93.9 %shard_map.86 = (bf16[1,256,2048]{2,1,0:T(8,128)(2,1)S(1)}, bf16[1,256,1024]{2,1,0:T(8,128)(2,1)S(1)}) custom-call(bf16[1,256,2048]{2,1,0:T(8,128)(2,1)S(1)} %copy-done, bf16[1,256,1024]{2,1,0:T(8,128)(2,1)S(1)} %copy-done.1, bf16[1,256,1024]{2,1,0:T(8,128)(2,1)S(1)} %copy-done.2, s32[1,7]{1,0:T(1,128)S(1)} %copy-done.5, s32[16,7,2]{2,1,0:T(8,128)S(1)} %copy.9.refs_4_, ...), custom_call_target="tpu_custom_call" | custom-call | tf_op jit(solution)/shard_map/pallas_call | solution.py:380
  99.7 1.0 copy.12
  100.7 0.8 copy.13
Async XLA Ops:
  0.6 0.9 copy-start.4
  0.6 0.8 copy-start.5
  1.5 1.2 %copy-start = (bf16[1,256,2048]{2,1,0:T(8,128)(2,1)S(1)}, bf16[1,256,2048]{2,1,0:T(8,128)(2,1)}, u32[]{:S(2)}) copy-start(bf16[1,256,2048]{2,1,0:T(8,128)(2,1)} %refs_0_.1) | copy-start | bytes 3145732
  2.7 1.0 %copy-start.1 = (bf16[1,256,1024]{2,1,0:T(8,128)(2,1)S(1)}, bf16[1,256,1024]{2,1,0:T(8,128)(2,1)}, u32[]{:S(2)}) copy-start(bf16[1,256,1024]{2,1,0:T(8,128)(2,1)} %refs_1_.1) | copy-start | bytes 1572868
  3.8 1.0 %copy-start.2 = (bf16[1,256,1024]{2,1,0:T(8,128)(2,1)S(1)}, bf16[1,256,1024]{2,1,0:T(8,128)(2,1)}, u32[]{:S(2)}) copy-start(bf16[1,256,1024]{2,1,0:T(8,128)(2,1)} %refs_2_.1) | copy-start | bytes 1572868
  4.8 1.0 %copy-start.3 = (bf16[8,16,2048]{2,1,0:T(8,128)(2,1)S(1)}, bf16[8,16,2048]{2,1,0:T(8,128)(2,1)}, u32[]{:S(2)}) copy-start(bf16[8,16,2048]{2,1,0:T(8,128)(2,1)} %refs_5_.1) | copy-start | bytes 1572868

commit v2 on v1

--- a/solution.py
+++ b/solution.py
@@ -36,6 +36,8 @@
     freq,
     attended,
     cache,
+    qraw,
+    kraw,
     qrot,
     krot,
     qbuf,
@@ -97,9 +99,13 @@
     own_v = pltpu.make_async_copy(
         values.at[0, :, lanes(z, HEAD)], kvbuf.at[rows(RING + z), HEAD:PAIR], local.at[2]
     )
+    load_k = pltpu.make_async_copy(keys.at[0], kraw, local.at[5])
+    load_q = pltpu.make_async_copy(queries.at[0], qraw, local.at[6])
+    load_k.start()
     own_pool_k.start()
     own_pool_v.start()
     own_v.start()
+    load_q.start()
     pl.semaphore_wait(barrier, RING - 1 + 2 + n_batch - 1)
 
     def send_v(d):
@@ -162,8 +168,8 @@
             device_id_type=MESH,
         )
 
-    near = (1, 7, 2, 6, 3, 5, 4)
-    for d in near:
+    order = (4, 3, 5, 2, 6, 1, 7)
+    for d in order:
         send_v(d).start()
     own_pool_k.wait()
     own_pool_v.wait()
@@ -198,9 +204,10 @@
         part = part.astype(jnp.float32)
         return (part * cosine + pltpu.roll(part, HEAD // 2, 1) * sine).astype(jnp.bfloat16)
 
+    load_k.wait()
     for h in range(KV_HEADS):
-        krot[:, h * HEAD : (h + 1) * HEAD] = turn(keys[0, :, h * HEAD : (h + 1) * HEAD])
-    for d in near:
+        krot[:, h * HEAD : (h + 1) * HEAD] = turn(kraw[:, h * HEAD : (h + 1) * HEAD])
+    for d in order:
         send_k(d).start()
     own_k = pltpu.make_async_copy(
         krot.at[:, lanes(z, HEAD)], kvbuf.at[rows(RING + z), 0:HEAD], local.at[1]
@@ -208,9 +215,10 @@
     own_k.start()
     cache_copy = pltpu.make_async_copy(krot, cache.at[0], local.at[3])
     cache_copy.start()
+    load_q.wait()
     for h in range(2 * KV_HEADS):
-        qrot[:, h * HEAD : (h + 1) * HEAD] = turn(queries[0, :, h * HEAD : (h + 1) * HEAD])
-    for d in near:
+        qrot[:, h * HEAD : (h + 1) * HEAD] = turn(qraw[:, h * HEAD : (h + 1) * HEAD])
+    for d in order:
         send_q(d).start()
     own_q = pltpu.make_async_copy(qrot.at[:, lanes(z, PAIR)], qbuf.at[z], local.at[4])
     own_q.start()
@@ -231,7 +239,7 @@
             device_id_type=MESH,
         )
 
-    for d in near:
+    for d in order:
         from_ring(v_recv, HEAD, d).wait_recv()
         from_ring(k_recv, 0, d).wait_recv()
         forward(ring(RING - d)).start()
@@ -263,14 +271,14 @@
     def one_block(i, carry):
         odd = lax.rem(i, 2)
         half = lax.div(i + 1, 2)
-        d = lax.rem(odd * half + (1 - odd) * (RING - half), RING)
+        d = RING // 2 + (1 - 2 * odd) * half
         src = ring(RING - d)
 
-        @pl.when(i == 0)
+        @pl.when(d == 0)
         def _():
             pltpu.make_async_copy(qrot.at[:, lanes(z, PAIR)], qbuf.at[z], local.at[4]).wait()
 
-        @pl.when(i > 0)
+        @pl.when(d > 0)
         def _():
             pltpu.make_async_remote_copy(
                 src_ref=qbuf.at[src],
@@ -325,13 +333,13 @@
         obuf[d, :, 0:HEAD] = result[0:TOK]
         obuf[d, :, HEAD:PAIR] = result[TOK : 2 * TOK]
 
-        @pl.when(i == 0)
+        @pl.when(d == 0)
         def _():
             pltpu.make_async_copy(
                 obuf.at[0], attended.at[0, :, lanes(z, PAIR)], local.at[2]
             ).start()
 
-        @pl.when(i > 0)
+        @pl.when(d > 0)
         def _():
             send_o(d).start()
 
@@ -383,9 +391,11 @@
             jax.ShapeDtypeStruct(queries.shape, bf),
             jax.ShapeDtypeStruct(keys.shape, bf),
         ),
-        in_specs=[vmem, vmem, anywhere, smem, smem, anywhere, vmem],
+        in_specs=[anywhere, anywhere, anywhere, smem, smem, anywhere, vmem],
         out_specs=(anywhere, anywhere),
         scratch_shapes=[
+            pltpu.VMEM((TOK, 2 * KV_HEADS * HEAD), bf),
+            pltpu.VMEM((TOK, KV_HEADS * HEAD), bf),
             pltpu.VMEM((TOK, 2 * KV_HEADS * HEAD), bf),
             pltpu.VMEM((TOK, KV_HEADS * HEAD), bf),
             pltpu.VMEM((RING, TOK, PAIR), bf),
@@ -408,10 +418,10 @@
             dma((n_batch,)),
             dma((RING,)),
             dma((RING,)),
-            dma((5,)),
+            dma((7,)),
         ],
         compiler_params=pltpu.CompilerParams(
-            collective_id=0, has_side_effects=True, vmem_limit_bytes=48 * 1024 * 1024
+            collective_id=0, has_side_effects=True, vmem_limit_bytes=67043328
         ),
     )(queries, keys, values, lengths, page_table, pool, freq)
 

time: 103 us -> 95.6 us (0.928)
  Pallas kernels: 93.9 us -> 88.7 us
  local copies, waits for them, and re-layouts: 6.94 us -> 4.59 us
    pallas_call x1, Pallas kernels: 93.9 us -> 88.7 us  [per_device(): pl.pallas_call(body, out_shape=(jax.ShapeDtypeStruct(queries.shape, bf),...]
    unnamed x15 -> x5, local copies, waits for them, and re-layouts: 6.94 us -> 4.59 us
where the time goes in v2:
time: 95.6 us; the launch traced here: 94 us
  Pallas kernels  88.7 us (93%)
  local copies, waits for them, and re-layouts  4.59 us (5%)
    pallas_call x1, Pallas kernels, per_device(): pl.pallas_call(body, out_shape=(jax.ShapeDtypeStruct(queries.shape, bf),...  88.7 us
    unnamed x5, local copies, waits for them, and re-layouts  4.59 us

profile of v2, /device:TPU:1, one launch (start us, length us, event | category | flops | bytes accessed | tf_op | source)
XLA Modules:
  0.0 94.0 jit_solution(9160830579317207311)
XLA Ops:
  0.6 1.4 %copy.9.refs_4_ = s32[16,7,2]{2,1,0:T(8,128)} copy(s32[16,7,2]{0,2,1:T(2,128)} %param.13) | data formatting | bytes 1792 | tf_op args[6]
  2.1 88.7 %shard_map.86 = (bf16[1,256,2048]{2,1,0:T(8,128)(2,1)}, bf16[1,256,1024]{2,1,0:T(8,128)(2,1)}) custom-call(bf16[1,256,2048]{2,1,0:T(8,128)(2,1)} %refs_0_.1, bf16[1,256,1024]{2,1,0:T(8,128)(2,1)} %refs_1_.1, bf16[1,256,1024]{2,1,0:T(8,128)(2,1)} %refs_2_.1, s32[1,7]{1,0:T(1,128)} %refs_3_.1, s32[16,7,2]{2,1,0:T(8,128)} %copy.9.refs_4_, ...), custom_call_target="tpu_custom_call" | custom-call | tf_op jit(solution)/shard_map/pallas_call | solution.py:388
  90.8 0.0 copy-start
  90.8 2.4 %copy.12 = bf16[1,256,2048]{2,1,0:T(8,128)(2,1)} copy(bf16[1,256,2048]{2,1,0:T(8,128)(2,1)} %get-tuple-element.4) | data formatting | bytes 2097152
  93.2 0.0 copy-done
  93.2 0.8 copy.13
Async XLA Ops:
  90.8 2.4 %copy-start = (bf16[1,256,1024]{2,1,0:T(8,128)(2,1)S(1)}, bf16[1,256,1024]{2,1,0:T(8,128)(2,1)}, u32[]{:S(2)}) copy-start(bf16[1,256,1024]{2,1,0:T(8,128)(2,1)} %get-tuple-element.5) | copy-start | bytes 1572868

commit v3 on v2

--- a/solution.py
+++ b/solution.py
@@ -40,8 +40,10 @@
     kraw,
     qrot,
     krot,
+    vown,
     qbuf,
-    kvbuf,
+    kbuf,
+    vbuf,
     pbuf,
     pown,
     pre,
@@ -54,13 +56,16 @@
     k_recv,
     q_send,
     q_recv,
-    f_send,
-    f_recv,
+    fv_send,
+    fv_recv,
+    fk_send,
+    fk_recv,
     p_send,
     p_recv,
     o_send,
     o_recv,
     local,
+    v_load,
 ):
     blk = lax.axis_index("blk")
     bat = lax.axis_index("batch")
@@ -96,22 +101,24 @@
     own_pool_v = pltpu.make_async_copy(
         pool.at[:, :, lanes(z + KV_HEADS, HEAD)], pown.at[:, :, HEAD:PAIR], local.at[1]
     )
-    own_v = pltpu.make_async_copy(
-        values.at[0, :, lanes(z, HEAD)], kvbuf.at[rows(RING + z), HEAD:PAIR], local.at[2]
-    )
+    load_v = [
+        pltpu.make_async_copy(values.at[0, :, h * HEAD : (h + 1) * HEAD], vown.at[h], v_load.at[h])
+        for h in range(KV_HEADS)
+    ]
     load_k = pltpu.make_async_copy(keys.at[0], kraw, local.at[5])
     load_q = pltpu.make_async_copy(queries.at[0], qraw, local.at[6])
+    for copy in load_v:
+        copy.start()
     load_k.start()
     own_pool_k.start()
     own_pool_v.start()
-    own_v.start()
     load_q.start()
     pl.semaphore_wait(barrier, RING - 1 + 2 + n_batch - 1)
 
     def send_v(d):
         return pltpu.make_async_remote_copy(
-            src_ref=values.at[0, :, lanes(ring(d), HEAD)],
-            dst_ref=kvbuf.at[rows(RING + z), HEAD:PAIR],
+            src_ref=vown.at[ring(d)],
+            dst_ref=vbuf.at[rows(RING + z)],
             send_sem=v_send.at[d],
             recv_sem=v_recv.at[d],
             device_id=ring_id(d),
@@ -120,8 +127,8 @@
 
     def send_k(d):
         return pltpu.make_async_remote_copy(
-            src_ref=krot.at[:, lanes(ring(d), HEAD)],
-            dst_ref=kvbuf.at[rows(RING + z), 0:HEAD],
+            src_ref=krot.at[ring(d)],
+            dst_ref=kbuf.at[rows(RING + z)],
             send_sem=k_send.at[d],
             recv_sem=k_recv.at[d],
             device_id=ring_id(d),
@@ -130,7 +137,7 @@
 
     def send_q(d):
         return pltpu.make_async_remote_copy(
-            src_ref=qrot.at[:, lanes(ring(d), PAIR)],
+            src_ref=qrot.at[ring(d)],
             dst_ref=qbuf.at[z],
             send_sem=q_send.at[d],
             recv_sem=q_recv.at[d],
@@ -148,20 +155,26 @@
             device_id_type=MESH,
         )
 
-    def forward(s):
-        return pltpu.make_async_remote_copy(
-            src_ref=kvbuf.at[rows(RING + s)],
-            dst_ref=kvbuf.at[rows(s)],
-            send_sem=f_send.at[s],
-            recv_sem=f_recv.at[s],
+    def forward(buf, sends, recvs, s, src=None):
+        return pltpu.make_async_remote_copy(
+            src_ref=buf.at[rows(RING + s)] if src is None else src,
+            dst_ref=buf.at[rows(s)],
+            send_sem=sends.at[s],
+            recv_sem=recvs.at[s],
             device_id=ahead,
             device_id_type=MESH,
         )
 
+    def forward_v(s, src=None):
+        return forward(vbuf, fv_send, fv_recv, s, src)
+
+    def forward_k(s, src=None):
+        return forward(kbuf, fk_send, fk_recv, s, src)
+
     def send_o(d):
         return pltpu.make_async_remote_copy(
             src_ref=obuf.at[d],
-            dst_ref=attended.at[0, :, lanes(z, PAIR)],
+            dst_ref=attended.at[z],
             send_sem=o_send.at[d],
             recv_sem=o_recv.at[d],
             device_id=ring_id(RING - d),
@@ -169,8 +182,13 @@
         )
 
     order = (4, 3, 5, 2, 6, 1, 7)
+    for copy in load_v:
+        copy.wait()
     for d in order:
         send_v(d).start()
+    own_v = pltpu.make_async_copy(vown.at[z], vbuf.at[rows(RING + z)], local.at[2])
+    own_v.start()
+    forward_v(z, vown.at[z]).start()
     own_pool_k.wait()
     own_pool_v.wait()
     for e in range(1, n_batch):
@@ -206,43 +224,42 @@
 
     load_k.wait()
     for h in range(KV_HEADS):
-        krot[:, h * HEAD : (h + 1) * HEAD] = turn(kraw[:, h * HEAD : (h + 1) * HEAD])
+        krot[h] = turn(kraw[:, h * HEAD : (h + 1) * HEAD])
     for d in order:
         send_k(d).start()
-    own_k = pltpu.make_async_copy(
-        krot.at[:, lanes(z, HEAD)], kvbuf.at[rows(RING + z), 0:HEAD], local.at[1]
-    )
+    own_k = pltpu.make_async_copy(krot.at[z], kbuf.at[rows(RING + z)], local.at[1])
     own_k.start()
-    cache_copy = pltpu.make_async_copy(krot, cache.at[0], local.at[3])
+    forward_k(z, krot.at[z]).start()
+    cache_copy = pltpu.make_async_copy(krot, cache, local.at[3])
     cache_copy.start()
     load_q.wait()
     for h in range(2 * KV_HEADS):
-        qrot[:, h * HEAD : (h + 1) * HEAD] = turn(qraw[:, h * HEAD : (h + 1) * HEAD])
+        at = (h % 2) * HEAD
+        qrot[h // 2, :, at : at + HEAD] = turn(qraw[:, h * HEAD : (h + 1) * HEAD])
     for d in order:
         send_q(d).start()
-    own_q = pltpu.make_async_copy(qrot.at[:, lanes(z, PAIR)], qbuf.at[z], local.at[4])
+    own_q = pltpu.make_async_copy(qrot.at[z], qbuf.at[z], local.at[4])
     own_q.start()
 
-    own_v.wait()
-    own_k.wait()
-    forward(z).start()
-
-    def from_ring(sem, width_lo, d):
-        src = ring(RING - d)
-        view = kvbuf.at[rows(RING + src), width_lo : width_lo + HEAD]
+    def from_ring(buf, recvs, d):
+        view = buf.at[rows(RING + ring(RING - d))]
         return pltpu.make_async_remote_copy(
             src_ref=view,
             dst_ref=view,
             send_sem=v_send.at[d],
-            recv_sem=sem.at[d],
+            recv_sem=recvs.at[d],
             device_id=ring_id(RING - d),
             device_id_type=MESH,
         )
 
     for d in order:
-        from_ring(v_recv, HEAD, d).wait_recv()
-        from_ring(k_recv, 0, d).wait_recv()
-        forward(ring(RING - d)).start()
+        from_ring(vbuf, v_recv, d).wait_recv()
+        forward_v(ring(RING - d)).start()
+    for d in order:
+        from_ring(kbuf, k_recv, d).wait_recv()
+        forward_k(ring(RING - d)).start()
+    own_v.wait()
+    own_k.wait()
 
     own_pool.wait()
     for e in range(1, n_batch):
@@ -258,11 +275,12 @@
     for s in range(SEGS):
         for i in range(PAGES_SEG):
             at = s * PREFIX + i * PAGE
-            pre[at : at + PAGE, :] = pbuf[page_table[bat, s, i]]
+            pre[at : at + PAGE, :] = pbuf[page_table[s, i, bat]]
     pre[SEGS * PREFIX :, :] = jnp.zeros((TOK - SEGS * PREFIX, PAIR), jnp.bfloat16)
 
     for s in range(RING):
-        forward(s).wait_recv()
+        forward_v(s).wait_recv()
+        forward_k(s).wait_recv()
 
     row2 = lax.rem(lax.broadcasted_iota(jnp.int32, (2 * TOK, HEAD), 0), TOK)
     lane2 = lax.broadcasted_iota(jnp.int32, (2 * TOK, HEAD), 1)
@@ -276,7 +294,7 @@
 
         @pl.when(d == 0)
         def _():
-            pltpu.make_async_copy(qrot.at[:, lanes(z, PAIR)], qbuf.at[z], local.at[4]).wait()
+            pltpu.make_async_copy(qrot.at[z], qbuf.at[z], local.at[4]).wait()
 
         @pl.when(d > 0)
         def _():
@@ -299,7 +317,7 @@
         highest = jnp.full((2 * TOK, HEAD), NEG, jnp.float32)
         for c in range(RING + 2):
             if c <= RING:
-                tile = kvbuf[rows(src + c), 0:HEAD]
+                tile = kbuf[rows(src + c), :]
             else:
                 tile = pre[:, 0:HEAD]
             score = lax.dot_general(
@@ -323,7 +341,7 @@
             weight = jnp.exp2((scores[c] - top) * LOG2E_SCALE)
             total = total + (weight[:, 0:HEAD] + weight[:, HEAD:PAIR])
             if c <= RING:
-                tile = kvbuf[rows(src + c), HEAD:PAIR]
+                tile = vbuf[rows(src + c), :]
             else:
                 tile = pre[:, HEAD:PAIR]
             summed = summed + jnp.dot(
@@ -336,7 +354,7 @@
         @pl.when(d == 0)
         def _():
             pltpu.make_async_copy(
-                obuf.at[0], attended.at[0, :, lanes(z, PAIR)], local.at[2]
+                obuf.at[0], attended.at[z], local.at[2]
             ).start()
 
         @pl.when(d > 0)
@@ -352,21 +370,48 @@
         send_k(d).wait_send()
         send_q(d).wait_send()
     for s in range(RING):
-        forward(s).wait_send()
+        forward_v(s).wait_send()
+        forward_k(s).wait_send()
     for e in range(1, n_batch):
         send_pool(e).wait_send()
     cache_copy.wait()
-    pltpu.make_async_copy(obuf.at[0], attended.at[0, :, lanes(z, PAIR)], local.at[2]).wait()
+    pltpu.make_async_copy(obuf.at[0], attended.at[z], local.at[2]).wait()
     for d in range(1, RING):
         send_o(d).wait_send()
         pltpu.make_async_remote_copy(
             src_ref=obuf.at[d],
-            dst_ref=attended.at[0, :, lanes(ring(d), PAIR)],
+            dst_ref=attended.at[ring(d)],
             send_sem=o_send.at[d],
             recv_sem=o_recv.at[d],
             device_id=ring_id(d),
             device_id_type=MESH,
         ).wait_recv()
+
+
+def finish(heads, rotated, attended, cache, h_buf, r_buf, h_in, r_in, h_out, r_out):
+    loads = []
+    for s in range(KV_HEADS):
+        loads.append(pltpu.make_async_copy(heads.at[s], h_buf.at[s], h_in.at[s]))
+        loads.append(pltpu.make_async_copy(rotated.at[s], r_buf.at[s], r_in.at[s]))
+    for copy in loads:
+        copy.start()
+    stores = []
+    for s in range(KV_HEADS):
+        stores.append(
+            pltpu.make_async_copy(
+                h_buf.at[s], attended.at[0, :, s * PAIR : (s + 1) * PAIR], h_out.at[s]
+            )
+        )
+        stores.append(
+            pltpu.make_async_copy(
+                r_buf.at[s], cache.at[0, :, s * HEAD : (s + 1) * HEAD], r_out.at[s]
+            )
+        )
+    for load, store in zip(loads, stores):
+        load.wait()
+        store.start()
+    for copy in stores:
+        copy.wait()
 
 
 def per_device(queries, keys, values, seg_ids, lengths, live, page_table, pool):
@@ -385,21 +430,23 @@
     vmem = pl.BlockSpec(memory_space=pltpu.VMEM)
     smem = pl.BlockSpec(memory_space=pltpu.SMEM)
     anywhere = pl.BlockSpec(memory_space=pl.ANY)
-    return pl.pallas_call(
+    heads, rotated = pl.pallas_call(
         body,
         out_shape=(
-            jax.ShapeDtypeStruct(queries.shape, bf),
-            jax.ShapeDtypeStruct(keys.shape, bf),
+            jax.ShapeDtypeStruct((KV_HEADS, TOK, PAIR), bf),
+            jax.ShapeDtypeStruct((KV_HEADS, TOK, HEAD), bf),
         ),
         in_specs=[anywhere, anywhere, anywhere, smem, smem, anywhere, vmem],
         out_specs=(anywhere, anywhere),
         scratch_shapes=[
             pltpu.VMEM((TOK, 2 * KV_HEADS * HEAD), bf),
             pltpu.VMEM((TOK, KV_HEADS * HEAD), bf),
-            pltpu.VMEM((TOK, 2 * KV_HEADS * HEAD), bf),
-            pltpu.VMEM((TOK, KV_HEADS * HEAD), bf),
+            pltpu.VMEM((KV_HEADS, TOK, PAIR), bf),
+            pltpu.VMEM((KV_HEADS, TOK, HEAD), bf),
+            pltpu.VMEM((KV_HEADS, TOK, HEAD), bf),
             pltpu.VMEM((RING, TOK, PAIR), bf),
-            pltpu.VMEM((2 * RING * TOK, PAIR), bf),
+            pltpu.VMEM((2 * RING * TOK, HEAD), bf),
+            pltpu.VMEM((2 * RING * TOK, HEAD), bf),
             pltpu.VMEM((n_batch * pool_rows, PAGE, PAIR), bf),
             pltpu.VMEM((pool_rows, PAGE, PAIR), bf),
             pltpu.VMEM((TOK, PAIR), bf),
@@ -414,16 +461,37 @@
             dma((RING,)),
             dma((RING,)),
             dma((RING,)),
+            dma((RING,)),
+            dma((RING,)),
             dma((n_batch,)),
             dma((n_batch,)),
             dma((RING,)),
             dma((RING,)),
             dma((7,)),
+            dma((KV_HEADS,)),
         ],
         compiler_params=pltpu.CompilerParams(
             collective_id=0, has_side_effects=True, vmem_limit_bytes=67043328
         ),
-    )(queries, keys, values, lengths, page_table, pool, freq)
+    )(queries, keys, values, lengths, jnp.transpose(page_table, (1, 2, 0)), pool, freq)
+    return pl.pallas_call(
+        finish,
+        out_shape=(
+            jax.ShapeDtypeStruct(queries.shape, bf),
+            jax.ShapeDtypeStruct(keys.shape, bf),
+        ),
+        in_specs=[anywhere, anywhere],
+        out_specs=(anywhere, anywhere),
+        scratch_shapes=[
+            pltpu.VMEM((KV_HEADS, TOK, PAIR), bf),
+            pltpu.VMEM((KV_HEADS, TOK, HEAD), bf),
+            dma((KV_HEADS,)),
+            dma((KV_HEADS,)),
+            dma((KV_HEADS,)),
+            dma((KV_HEADS,)),
+        ],
+        compiler_params=pltpu.CompilerParams(vmem_limit_bytes=67043328),
+    )(heads, rotated)
 
 
 def solution(mesh):

time: 95.6 us -> 90.6 us (0.948); the launches traced: 94 us -> 90.4 us
  local copies, waits for them, and re-layouts: 4.59 us -> 0 us
  Pallas kernels: 88.7 us -> 89.8 us
    unnamed x5 -> x0, local copies, waits for them, and re-layouts: 4.59 us -> none
    pallas_call x1 -> x2, Pallas kernels: 88.7 us -> 89.8 us  [the longest x1 87.4 us: per_device(): pl.pallas_call(body, out_shape=(jax.ShapeDtypeStruct((KV_HEADS, TOK, PAIR...]
where the time goes in v3:
time: 90.6 us; the launch traced here: 90.4 us
  Pallas kernels  89.8 us (99%)
    pallas_call x1, Pallas kernels, per_device(): pl.pallas_call(body, out_shape=(jax.ShapeDtypeStruct((KV_HEADS, TOK, PAIR...  87.4 us
    pallas_call x1, Pallas kernels, per_device(): pl.pallas_call(finish, out_shape=(jax.ShapeDtypeStruct(queries.shape, bf)...  2.39 us

profile of v3, /device:TPU:1, one launch (start us, length us, event | category | flops | bytes accessed | tf_op | source)
XLA Modules:
  0.0 90.4 jit_solution(2705872902268263260)
XLA Ops:
  0.6 87.4 %shard_map.86 = (bf16[8,256,256]{2,1,0:T(8,128)(2,1)}, bf16[8,256,128]{2,1,0:T(8,128)(2,1)}) custom-call(bf16[1,256,2048]{2,1,0:T(8,128)(2,1)} %refs_0_.1, bf16[1,256,1024]{2,1,0:T(8,128)(2,1)} %refs_1_.1, bf16[1,256,1024]{2,1,0:T(8,128)(2,1)} %refs_2_.1, s32[1,7]{1,0:T(1,128)} %refs_3_.1, s32[7,2,16]{2,1,0:T(2,128)} %bitcast.1, ...), custom_call_target="tpu_custom_call" | custom-call | tf_op jit(solution)/shard_map/pallas_call | solution.py:433
  88.0 2.4 %shard_map.87 = (bf16[1,256,2048]{2,1,0:T(8,128)(2,1)}, bf16[1,256,1024]{2,1,0:T(8,128)(2,1)}) custom-call(bf16[8,256,256]{2,1,0:T(8,128)(2,1)} %get-tuple-element.4.heads, bf16[8,256,128]{2,1,0:T(8,128)(2,1)} %get-tuple-element.5.rotated), custom_call_target="tpu_custom_call" | custom-call | tf_op jit(solution)/shard_map/pallas_call | solution.py:477

commit v4 on v3

--- a/solution.py
+++ b/solution.py
@@ -101,14 +101,16 @@
     own_pool_v = pltpu.make_async_copy(
         pool.at[:, :, lanes(z + KV_HEADS, HEAD)], pown.at[:, :, HEAD:PAIR], local.at[1]
     )
-    load_v = [
-        pltpu.make_async_copy(values.at[0, :, h * HEAD : (h + 1) * HEAD], vown.at[h], v_load.at[h])
-        for h in range(KV_HEADS)
-    ]
+    def load_v(d):
+        return pltpu.make_async_copy(
+            values.at[0, :, lanes(ring(d), HEAD)], vown.at[ring(d)], v_load.at[d]
+        )
+
+    order = (4, 3, 5, 2, 6, 1, 7)
     load_k = pltpu.make_async_copy(keys.at[0], kraw, local.at[5])
     load_q = pltpu.make_async_copy(queries.at[0], qraw, local.at[6])
-    for copy in load_v:
-        copy.start()
+    for d in order + (0,):
+        load_v(d).start()
     load_k.start()
     own_pool_k.start()
     own_pool_v.start()
@@ -181,11 +183,10 @@
             device_id_type=MESH,
         )
 
-    order = (4, 3, 5, 2, 6, 1, 7)
-    for copy in load_v:
-        copy.wait()
     for d in order:
+        load_v(d).wait()
         send_v(d).start()
+    load_v(0).wait()
     own_v = pltpu.make_async_copy(vown.at[z], vbuf.at[rows(RING + z)], local.at[2])
     own_v.start()
     forward_v(z, vown.at[z]).start()
@@ -282,8 +283,6 @@
         forward_v(s).wait_recv()
         forward_k(s).wait_recv()
 
-    row2 = lax.rem(lax.broadcasted_iota(jnp.int32, (2 * TOK, HEAD), 0), TOK)
-    lane2 = lax.broadcasted_iota(jnp.int32, (2 * TOK, HEAD), 1)
     contract_last = (((1,), (1,)), ((), ()))
 
     def one_block(i, carry):
@@ -310,11 +309,11 @@
         q2[0:TOK, :] = qbuf[src, :, 0:HEAD]
         q2[TOK : 2 * TOK, :] = qbuf[src, :, HEAD:PAIR]
         block0 = (x * RING + src) * TOK
-        begin, segment = start_and_segment(row2 + block0)
-        limit = begin - lane2 - (block0 - RING * TOK)
-        causal = row2 - lane2
-        segment_at = segment * PREFIX - lane2
-        highest = jnp.full((2 * TOK, HEAD), NEG, jnp.float32)
+        begin, segment = start_and_segment(row + block0)
+        limit = begin - lane - (block0 - RING * TOK)
+        causal = row - lane
+        segment_at = segment * PREFIX - lane
+        highest = [jnp.full((TOK, HEAD), NEG, jnp.float32)] * 2
         for c in range(RING + 2):
             if c <= RING:
                 tile = kbuf[rows(src + c), :]
@@ -331,10 +330,12 @@
                     seen = (limit <= c * TOK + at) & (causal >= at)
                 else:
                     seen = (segment_at <= at) & (segment_at > at - PREFIX)
-                piece = jnp.where(seen, score[:, at : at + HEAD], NEG)
-                highest = jnp.maximum(highest, piece)
-                scores[c, :, at : at + HEAD] = piece
-        top = jnp.max(highest, axis=1, keepdims=True)
+                for g in range(2):
+                    own = slice(g * TOK, (g + 1) * TOK)
+                    piece = jnp.where(seen, score[own, at : at + HEAD], NEG)
+                    highest[g] = jnp.maximum(highest[g], piece)
+                    scores[c, own, at : at + HEAD] = piece
+        top = jnp.concatenate([jnp.max(part, axis=1, keepdims=True) for part in highest], axis=0)
         total = jnp.zeros((2 * TOK, HEAD), jnp.float32)
         summed = jnp.zeros((2 * TOK, HEAD), jnp.float32)
         for c in range(RING + 2):

time: 90.6 us -> 90.6 us (level)
  no operation moved by 1% of the time
where the time goes in v4:
time: 90.6 us; the launch traced here: 90.4 us
  Pallas kernels  89.7 us (99%)
    pallas_call x1, Pallas kernels, per_device(): pl.pallas_call(body, out_shape=(jax.ShapeDtypeStruct((KV_HEADS, TOK, PAIR...  87.3 us
    pallas_call x1, Pallas kernels, per_device(): pl.pallas_call(finish, out_shape=(jax.ShapeDtypeStruct(queries.shape, bf)...  2.39 us

profile of v4, /device:TPU:1, one launch (start us, length us, event | category | flops | bytes accessed | tf_op | source)
XLA Modules:
  0.0 90.4 jit_solution(15255646765262524877)
XLA Ops:
  0.6 87.3 %shard_map.86 = (bf16[8,256,256]{2,1,0:T(8,128)(2,1)}, bf16[8,256,128]{2,1,0:T(8,128)(2,1)}) custom-call(bf16[1,256,2048]{2,1,0:T(8,128)(2,1)} %refs_0_.1, bf16[1,256,1024]{2,1,0:T(8,128)(2,1)} %refs_1_.1, bf16[1,256,1024]{2,1,0:T(8,128)(2,1)} %refs_2_.1, s32[1,7]{1,0:T(1,128)} %refs_3_.1, s32[7,2,16]{2,1,0:T(2,128)} %bitcast.1, ...), custom_call_target="tpu_custom_call" | custom-call | tf_op jit(solution)/shard_map/pallas_call | solution.py:434
  88.0 2.4 %shard_map.87 = (bf16[1,256,2048]{2,1,0:T(8,128)(2,1)}, bf16[1,256,1024]{2,1,0:T(8,128)(2,1)}) custom-call(bf16[8,256,256]{2,1,0:T(8,128)(2,1)} %get-tuple-element.4.heads, bf16[8,256,128]{2,1,0:T(8,128)(2,1)} %get-tuple-element.5.rotated), custom_call_target="tpu_custom_call" | custom-call | tf_op jit(solution)/shard_map/pallas_call | solution.py:478

commit v5 on v4

--- a/solution.py
+++ b/solution.py
@@ -107,9 +107,10 @@
         )
 
     order = (4, 3, 5, 2, 6, 1, 7)
+    near = (1, 7, 2, 6, 3, 5, 4)
     load_k = pltpu.make_async_copy(keys.at[0], kraw, local.at[5])
     load_q = pltpu.make_async_copy(queries.at[0], qraw, local.at[6])
-    for d in order + (0,):
+    for d in near + (0,):
         load_v(d).start()
     load_k.start()
     own_pool_k.start()
@@ -183,7 +184,7 @@
             device_id_type=MESH,
         )
 
-    for d in order:
+    for d in near:
         load_v(d).wait()
         send_v(d).start()
     load_v(0).wait()
@@ -226,7 +227,7 @@
     load_k.wait()
     for h in range(KV_HEADS):
         krot[h] = turn(kraw[:, h * HEAD : (h + 1) * HEAD])
-    for d in order:
+    for d in near:
         send_k(d).start()
     own_k = pltpu.make_async_copy(krot.at[z], kbuf.at[rows(RING + z)], local.at[1])
     own_k.start()
@@ -253,10 +254,10 @@
             device_id_type=MESH,
         )
 
-    for d in order:
+    for d in near:
         from_ring(vbuf, v_recv, d).wait_recv()
         forward_v(ring(RING - d)).start()
-    for d in order:
+    for d in near:
         from_ring(kbuf, k_recv, d).wait_recv()
         forward_k(ring(RING - d)).start()
     own_v.wait()

time: 90.6 us -> 91.8 us (1.013); the launches traced: 90.4 us -> 90.1 us
  no operation moved by 1% of the time
where the time goes in v5:
time: 91.8 us; the launch traced here: 90.1 us
  Pallas kernels  89.5 us (97%)
    pallas_call x1, Pallas kernels, per_device(): pl.pallas_call(body, out_shape=(jax.ShapeDtypeStruct((KV_HEADS, TOK, PAIR...  87.1 us
    pallas_call x1, Pallas kernels, per_device(): pl.pallas_call(finish, out_shape=(jax.ShapeDtypeStruct(queries.shape, bf)...  2.39 us

profile of v5, /device:TPU:1, one launch (start us, length us, event | category | flops | bytes accessed | tf_op | source)
XLA Modules:
  0.0 90.1 jit_solution(14972091924358249405)
XLA Ops:
  0.6 87.1 %shard_map.86 = (bf16[8,256,256]{2,1,0:T(8,128)(2,1)}, bf16[8,256,128]{2,1,0:T(8,128)(2,1)}) custom-call(bf16[1,256,2048]{2,1,0:T(8,128)(2,1)} %refs_0_.1, bf16[1,256,1024]{2,1,0:T(8,128)(2,1)} %refs_1_.1, bf16[1,256,1024]{2,1,0:T(8,128)(2,1)} %refs_2_.1, s32[1,7]{1,0:T(1,128)} %refs_3_.1, s32[7,2,16]{2,1,0:T(2,128)} %bitcast.1, ...), custom_call_target="tpu_custom_call" | custom-call | tf_op jit(solution)/shard_map/pallas_call | solution.py:435
  87.7 2.4 %shard_map.87 = (bf16[1,256,2048]{2,1,0:T(8,128)(2,1)}, bf16[1,256,1024]{2,1,0:T(8,128)(2,1)}) custom-call(bf16[8,256,256]{2,1,0:T(8,128)(2,1)} %get-tuple-element.4.heads, bf16[8,256,128]{2,1,0:T(8,128)(2,1)} %get-tuple-element.5.rotated), custom_call_target="tpu_custom_call" | custom-call | tf_op jit(solution)/shard_map/pallas_call | solution.py:479
